TPU v7x, 256 devices: a 8x8x2 block of a 8x8x16 slice. The times are simulated.
256 devices in a mesh: replica: 2 (over z), expert: 64 (over y, x), sub: 2 (over core).
Axes of the slice: x: 8, y: 8, z: 2, core: 2. Of those that a mesh axis runs over, the one named last changes fastest.
The devices are a block of a 8x8x16 slice.
Arguments:
- tokens: bfloat16 [2048, 7168], P(('replica', 'expert', 'sub')), parts along dimension 0, may hold values from -6 to 6
- expert_ids: int32 [2048, 8], P(('replica', 'expert', 'sub')), parts along dimension 0, may hold values from 0 to 31, all different within a row; in each aligned block of 8 rows (0 to 7, 8 to 15, ...) at most 3 rows name the same one
- route_levels: int32 [2048, 8], P(('replica', 'expert', 'sub')), parts along dimension 0, may hold values from 1 to 255
- gate_proj: bfloat16 [64, 7168, 512], P('expert', None, 'sub'), may hold values from -0.0625 to 0.0625
- up_proj: bfloat16 [64, 7168, 512], P('expert', None, 'sub'), may hold values from -0.0625 to 0.0625
- down_proj: bfloat16 [64, 512, 7168], P('expert', 'sub'), may hold values from -0.1875 to 0.1875
Outputs:
- moe_out: bfloat16 [2048, 7168], P(('replica', 'expert', 'sub')), parts along dimension 0
There are 2 independent parts, one for each index of `replica`. A program takes and returns all parts, laid end to end along the dimension named above; an argument that names none is the same for every part. Nothing has to cross between parts.
Inputs may be any that keep to these rules, and one draw needn't show every extreme that they name: `expert_ids`: each row names 8 different experts; among the 8 rows of one device no expert is named more than 3 times, and in some devices' rows one is named exactly 3 times.
All inputs are finite; a program needn't handle non-finite values.
Results may differ from a plain program's by a relative error of at most 0.013.
Values may be sent and summed in bfloat16 or wider, within the bound.
A program may use at most 448 MiB of HBM per device.

v0:
```python
import jax
import jax.numpy as jnp
from jax import lax
from jax.sharding import PartitionSpec as P


def local(tokens, expert_ids, route_levels, gate_proj, up_proj, down_proj):
    rows, width = tokens.shape
    experts = lax.axis_size("expert") // 2
    levels = jnp.sum(
        jnp.where(
            expert_ids[:, :, None] == jnp.arange(128, dtype=jnp.int32), route_levels[:, :, None], 0
        ),
        axis=1,
    )
    carried = jnp.concatenate([tokens, levels.astype(jnp.bfloat16)], axis=1)
    everyone = lax.all_gather(carried, ("expert", "sub"), axis=0, tiled=True)
    x = everyone[:, :width]
    level = everyone[:, width:].astype(jnp.float32)
    mine = jnp.arange(128, dtype=jnp.int32) == lax.axis_index("expert") // 2
    share = jnp.sum(jnp.where(mine, level, 0.0), axis=1, keepdims=True) / jnp.sum(
        level, axis=1, keepdims=True
    )
    gate = jnp.dot(x, gate_proj[0], preferred_element_type=jnp.float32)
    up = jnp.dot(x, up_proj[0], preferred_element_type=jnp.float32)
    hidden = (jax.nn.silu(gate) * up * share).astype(jnp.bfloat16)
    part = jnp.dot(hidden, down_proj[0], preferred_element_type=jnp.float32).astype(jnp.bfloat16)
    return lax.psum_scatter(part, ("expert", "sub"), scatter_dimension=0, tiled=True)


def solution(mesh):
    return jax.shard_map(
        local,
        mesh=mesh,
        in_specs=(
            P(("replica", "expert", "sub"), None),
            P(("replica", "expert", "sub"), None),
            P(("replica", "expert", "sub"), None),
            P("expert", None, "sub"),
            P("expert", None, "sub"),
            P("expert", "sub", None),
        ),
        out_specs=P(("replica", "expert", "sub"), None),
        check_vma=False,
    )
```

profile of v0, /device:TPU:516, one launch (start us, length us, event | category | flops | bytes accessed | tf_op | source)
XLA Modules:
  0.0 367.1 jit_solution(16336927684279294206)
XLA Ops:
  6.5 0.0 all-gather.2.cloned.1.call-start
  6.6 0.8 select_reduce_fusion
  7.4 1.5 pad_maximum_fusion
  8.9 0.1 all-gather.2.cloned.1.call-update
  9.0 0.1 reduce-scatter.2.cloned.1.call-start
  9.1 111.0 %all-gather.2.cloned.1.call-done = bf16[1024,7296]{1,0:T(8,128)(2,1)} async-done(((bf16[8,7296]{1,0:T(8,128)(2,1)}), bf16[1024,7296]{1,0:T(8,128)(2,1)}) %all-gather.2.cloned.1.call-update) | async-done | bytes 14942224 | tf_op jit(solution)/shard_map/all_gather | solution.py:17
  120.1 1.2 convert_reduce_fusion
  121.3 0.0 copy-start.1
  121.3 8.5 %fusion.2 = f32[1024,256]{1,0:T(8,128)S(1)} fusion(bf16[1024,7296]{1,0:T(8,128)(2,1)} %all-gather.2.cloned.1.call-done, bf16[1,7168,256]{2,1,0:T(8,128)(2,1)} %param.9), kind=kOutput, calls=%fused_computation.3 | convolution fusion | flops 3758096384 | bytes 19398656 | tf_op jit(solution)/shard_map/dot_general | solution.py:24
  129.8 0.0 copy-done.1
  129.8 0.0 copy-start
  129.8 9.4 %fusion.17 = bf16[1024,256]{1,0:T(8,128)(2,1)S(1)} fusion(bf16[1,7168,256]{2,1,0:T(8,128)(2,1)S(1)} %copy-done.1, bf16[1024,7296]{1,0:T(8,128)(2,1)} %all-gather.2.cloned.1.call-done, f32[1024,256]{1,0:T(8,128)S(1)} %fusion.2, f32[1024]{0:T(1024)S(1)} %div.24), kind=kOutput, calls=%fused_computation.10 | convolution fusion | flops 3759931392 | bytes 19927040 | tf_op jit(solution)/shard_map/dot_general | solution.py:25
  139.1 0.0 copy-done
  139.2 7.4 %convolution_convert_fusion = bf16[1024,7168]{1,0:T(8,128)(2,1)} fusion(bf16[1024,256]{1,0:T(8,128)(2,1)S(1)} %fusion.17, bf16[1,256,7168]{2,1,0:T(8,128)(2,1)S(1)} %copy-done), kind=kOutput, calls=%fused_computation | convolution fusion | flops 3765436416 | bytes 18874368 | tf_op jit(solution)/shard_map/dot_general | solution.py:27
  146.5 0.1 reduce-scatter.2.cloned.1.call-update
  146.6 213.6 %reduce-scatter.2.cloned.1.call-done = bf16[8,7168]{1,0:T(8,128)(2,1)} async-done(((bf16[1024,7168]{1,0:T(8,128)(2,1)}), bf16[8,7168]{1,0:T(8,128)(2,1)}) %reduce-scatter.2.cloned.1.call-update) | async-done | bytes 114704 | tf_op jit(solution)/shard_map/reduce_scatter | solution.py:28
  (3 shorter events, 0.0 us)
Async XLA Ops:
  6.5 113.5 %all-gather.2.cloned.1.call-start = ((), (), s32[]{:S(2)}) async-start(), calls=%async_computation.1 | async-start | bytes 15058944 | tf_op jit(solution)/shard_map/all_gather | solution.py:17
  9.0 351.2 %reduce-scatter.2.cloned.1.call-start = ((), (), s32[]{:S(2)}) async-start(), calls=%async_computation.2 | async-start | bytes 14794752 | tf_op jit(solution)/shard_map/reduce_scatter | solution.py:28
  121.3 8.5 %copy-start.1 = (bf16[1,7168,256]{2,1,0:T(8,128)(2,1)S(1)}, bf16[1,7168,256]{2,1,0:T(8,128)(2,1)}, u32[]{:S(2)}) copy-start(bf16[1,7168,256]{2,1,0:T(8,128)(2,1)} %param.10) | copy-start | bytes 11010052
  129.8 9.4 %copy-start = (bf16[1,256,7168]{2,1,0:T(8,128)(2,1)S(1)}, bf16[1,256,7168]{2,1,0:T(8,128)(2,1)}, u32[]{:S(2)}) copy-start(bf16[1,256,7168]{2,1,0:T(8,128)(2,1)} %param.11) | copy-start | bytes 11010052
Sparse Core Ops, SparseCore 0:
  10.0 110.0 all-gather.1
  146.7 213.4 reduce-scatter.1
where the time goes:
time: 367 us
  waiting for transfers between devices  325 us (89%)
  matrix products  25.2 us (7%)
  between operations  13.5 us (4%)
    reduce_scatter x1, waiting for transfers between devices, local(): lax.psum_scatter(part, ('expert', 'sub'), scatter_dimension=0, tiled=True)  214 us
    all_gather x1, waiting for transfers between devices, local(): everyone = lax.all_gather(carried, ('expert', 'sub'), axis=0, tiled=True)  111 us
    dot_general x1, matrix products, local(): up = jnp.dot(x, up_proj[0], preferred_element_type=jnp.float32)  9.36 us
    dot_general x1, matrix products, local(): gate = jnp.dot(x, gate_proj[0], preferred_element_type=jnp.float32)  8.45 us
    dot_general x1, matrix products, local(): jnp.dot(hidden, down_proj[0], preferred_element_type=jnp.float32)  7.38 us
  transfers between devices with their start and end apart: 2, of which 2 were waited for; matrix products, arithmetic and copies ran while one was open for 0% of the time, Pallas kernels for 0%

commit v1 on v0

--- a/solution.py
+++ b/solution.py
@@ -2,6 +2,13 @@
 import jax.numpy as jnp
 from jax import lax
 from jax.sharding import PartitionSpec as P
+
+
+def samples_pair(array_here, mesh_name, k_dim):
+    frame_out = lax.all_to_all(
+        jnp.stack(lax.axis_size(mesh_name) * [array_here], axis=0), mesh_name, 0, 0
+    )
+    return jnp.concatenate(frame_out, k_dim)
 
 
 def local(tokens, expert_ids, route_levels, gate_proj, up_proj, down_proj):
@@ -14,7 +21,7 @@
         axis=1,
     )
     carried = jnp.concatenate([tokens, levels.astype(jnp.bfloat16)], axis=1)
-    everyone = lax.all_gather(carried, ("expert", "sub"), axis=0, tiled=True)
+    everyone = samples_pair(carried, ("expert", "sub"), 0)
     x = everyone[:, :width]
     level = everyone[:, width:].astype(jnp.float32)
     mine = jnp.arange(128, dtype=jnp.int32) == lax.axis_index("expert") // 2

time: 367 us -> 781 us (2.13)
  waiting for transfers between devices: 325 us -> 705 us
  starting transfers between devices: 0.07 us -> 27.5 us
    all_to_all x0 -> x1, waiting for transfers between devices: none -> 469 us  [samples_pair(): lax.all_to_all(jnp.stack(lax.axis_size(mesh_name) * [array_here], axis=0)...]
    all_gather x1 -> x0, waiting for transfers between devices: 111 us -> none  [local(): everyone = lax.all_gather(carried, ('expert', 'sub'), axis=0, tiled=True)]
    all_to_all x0 -> x1, starting transfers between devices: none -> 27.2 us  [samples_pair(): lax.all_to_all(jnp.stack(lax.axis_size(mesh_name) * [array_here], axis=0)...]
    reduce_scatter x1, waiting for transfers between devices: 214 us -> 236 us  [local(): lax.psum_scatter(part, ('expert', 'sub'), scatter_dimension=0, tiled=True)]
where the time goes in v1:
time: 781 us; the launch traced here: 780 us
  waiting for transfers between devices  705 us (90%)
  starting transfers between devices  27.5 us (4%)
  matrix products  25.2 us (3%)
  between operations  13.5 us (2%)
    all_to_all x1, waiting for transfers between devices, samples_pair(): lax.all_to_all(jnp.stack(lax.axis_size(mesh_name) * [array_here], axis=0)...  469 us
    reduce_scatter x1, waiting for transfers between devices, local(): lax.psum_scatter(part, ('expert', 'sub'), scatter_dimension=0, tiled=True)  236 us
    all_to_all x1, starting transfers between devices, samples_pair(): lax.all_to_all(jnp.stack(lax.axis_size(mesh_name) * [array_here], axis=0)...  27.2 us
  transfers between devices with their start and end apart: 2, of which 2 were waited for; matrix products, arithmetic and copies ran while one was open for 0% of the time, Pallas kernels for 0%

profile of v1, /device:TPU:516, one launch (start us, length us, event | category | flops | bytes accessed | tf_op | source)
XLA Modules:
  0.0 780.3 jit_solution(3678805634846786632)
XLA Ops:
  6.5 0.8 select_reduce_fusion
  7.4 0.9 pad_maximum_fusion
  8.3 6.2 stack.2
  14.5 27.2 %all-to-all-start = ((bf16[128,8,7296]{2,1,0:T(8,128)(2,1)}), bf16[128,8,7296]{2,1,0:T(8,128)(2,1)}, u32[]{:S(2)}, u32[]{:S(2)}) async-start(bf16[128,8,7296]{2,1,0:T(8,128)(2,1)} %stack.2), calls=%async_computation | async-start | bytes 29884416 | tf_op jit(solution)/shard_map/all_to_all | solution.py:8
  41.7 0.2 reduce-scatter.2.cloned.1.call-start
  42.0 469.2 %all-to-all-done = bf16[128,8,7296]{2,1,0:T(8,128)(2,1)} async-done(((bf16[128,8,7296]{2,1,0:T(8,128)(2,1)}), bf16[128,8,7296]{2,1,0:T(8,128)(2,1)}, u32[]{:S(2)}, u32[]{:S(2)}) %all-to-all-start) | async-done | bytes 14942240 | tf_op jit(solution)/shard_map/all_to_all | solution.py:8
  511.1 0.0 copy-start.1
  511.1 8.4 %fusion.2 = f32[1024,256]{1,0:T(8,128)S(1)} fusion(bf16[1024,7296]{1,0:T(8,128)(2,1)} %bitcast, bf16[1,7168,256]{2,1,0:T(8,128)(2,1)} %param.9), kind=kOutput, calls=%fused_computation.3 | convolution fusion | flops 3758096384 | bytes 19398656 | tf_op jit(solution)/shard_map/dot_general | solution.py:31
  519.6 1.2 convert_reduce_fusion
  520.8 0.0 copy-done.1
  520.8 0.0 copy-start
  520.8 9.4 %fusion.17 = bf16[1024,256]{1,0:T(8,128)(2,1)S(1)} fusion(bf16[1,7168,256]{2,1,0:T(8,128)(2,1)S(1)} %copy-done.1, bf16[1024,7296]{1,0:T(8,128)(2,1)} %bitcast, f32[1024,256]{1,0:T(8,128)S(1)} %fusion.2, f32[1024]{0:T(1024)S(1)} %div.24), kind=kOutput, calls=%fused_computation.10 | convolution fusion | flops 3759931392 | bytes 19927040 | tf_op jit(solution)/shard_map/dot_general | solution.py:32
  530.2 0.0 copy-done
  530.2 7.4 convolution_convert_fusion
  537.6 0.1 reduce-scatter.2.cloned.1.call-update
  537.6 235.8 %reduce-scatter.2.cloned.1.call-done = bf16[8,7168]{1,0:T(8,128)(2,1)} async-done(((bf16[1024,7168]{1,0:T(8,128)(2,1)}), bf16[8,7168]{1,0:T(8,128)(2,1)}) %reduce-scatter.2.cloned.1.call-update) | async-done | bytes 114704 | tf_op jit(solution)/shard_map/reduce_scatter | solution.py:35
  (3 shorter events, 0.0 us)
Async XLA Ops:
  14.5 496.7 %all-to-all-start = ((bf16[128,8,7296]{2,1,0:T(8,128)(2,1)}), bf16[128,8,7296]{2,1,0:T(8,128)(2,1)}, u32[]{:S(2)}, u32[]{:S(2)}) async-start(bf16[128,8,7296]{2,1,0:T(8,128)(2,1)} %stack.2), calls=%async_computation | async-start | bytes 29884416 | tf_op jit(solution)/shard_map/all_to_all | solution.py:8
  41.7 731.7 %reduce-scatter.2.cloned.1.call-start = ((), (), s32[]{:S(2)}) async-start(), calls=%async_computation.2 | async-start | bytes 14794752 | tf_op jit(solution)/shard_map/reduce_scatter | solution.py:35
  511.1 9.7 %copy-start.1 = (bf16[1,7168,256]{2,1,0:T(8,128)(2,1)S(1)}, bf16[1,7168,256]{2,1,0:T(8,128)(2,1)}, u32[]{:S(2)}) copy-start(bf16[1,7168,256]{2,1,0:T(8,128)(2,1)} %param.10) | copy-start | bytes 11010052
  520.8 9.4 %copy-start = (bf16[1,256,7168]{2,1,0:T(8,128)(2,1)S(1)}, bf16[1,256,7168]{2,1,0:T(8,128)(2,1)}, u32[]{:S(2)}) copy-start(bf16[1,256,7168]{2,1,0:T(8,128)(2,1)} %param.11) | copy-start | bytes 11010052
Sparse Core Ops, SparseCore 0:
  537.8 235.6 reduce-scatter.1
